TPU v7x, 32 devices: a whole 2x2x4 slice. The times are simulated.
32 devices in a mesh: row: 4 (over z), col: 8 (over y, x, core).
Axes of the slice: x: 2, y: 2, z: 4, core: 2. Of those that a mesh axis runs over, the one named last changes fastest.
Arguments:
- rho_real: float32 [4096, 4096], P('row', 'col'), may hold values from -2.5 to 4, as said below
- rho_imag: float32 [4096, 4096], P('row', 'col'), may hold values from -2.5 to 2.5, as said below
- hamiltonian: bfloat16 [4096, 4096], P('row', 'col'), may hold values from -1 to 1
- amplitudes: float32 [8, 4096], replicated, may hold values from 0.15 to 0.6
- offsets: int32 [8], replicated, may hold values from -16 to 16
- active_jumps: int32 [1], replicated, may hold values from 4 to 8
Outputs:
- rho_next_real: float32 [4096, 4096], P('row', 'col')
- rho_next_imag: float32 [4096, 4096], P('row', 'col')
Inputs may be any that keep to these rules, and one draw needn't show every extreme that they name: `rho_real`: symmetric, with every diagonal entry 0.5 or more. `rho_imag`: antisymmetric.
All inputs are finite; a program needn't handle non-finite values.
Results may differ from a plain program's by a relative error of at most 0.001.
Values may be sent and summed in bfloat16 or wider, within the bound.
A program may use at most 192 MiB of HBM per device.

v0:
```python
import jax
import jax.numpy as jnp
from jax import lax
from jax.sharding import PartitionSpec as P

OMAX = 16
step_size = 0.25


def extended(cells, sides, width):
    for axis, dim in sides:
        count = lax.axis_size(axis)
        ends = count - 1
        head = lax.slice_in_dim(cells, 0, width, axis=dim)
        tail = lax.slice_in_dim(cells, cells.shape[dim] - width, cells.shape[dim], axis=dim)
        cells = jnp.concatenate(
            [
                lax.ppermute(tail, axis, [(i, (i + 1) % count) for i in range(ends)]),
                cells,
                lax.ppermute(head, axis, [((i + 1) % count, i) for i in range(ends)]),
            ],
            axis=dim,
        )
    return cells


def dissipate(matrix, padded, amplitudes, offsets, active, row_first, col_first):
    height = matrix.shape[1]
    breadth = matrix.shape[2]
    levels = amplitudes.shape[1]
    margin = (padded.shape[1] - height) // 2
    positions = jnp.arange(levels, dtype=jnp.int32)
    summed = jnp.zeros(matrix.shape, matrix.dtype)
    for jump_slot in range(amplitudes.shape[0]):
        offset = offsets[jump_slot]
        inside = (positions + offset >= 0) & (positions + offset < levels)
        strength = jnp.where(inside, amplitudes[jump_slot], 0.0)
        outflow = jnp.pad(strength * strength, (margin, margin))
        outflow = lax.dynamic_slice_in_dim(outflow, margin - offset, levels)
        row_strength = lax.dynamic_slice_in_dim(strength, row_first, height)
        col_strength = lax.dynamic_slice_in_dim(strength, col_first, breadth)
        row_outflow = lax.dynamic_slice_in_dim(outflow, row_first, height)
        col_outflow = lax.dynamic_slice_in_dim(outflow, col_first, breadth)
        corner = margin + offset
        shifted = lax.dynamic_slice(padded, (jnp.int32(0), corner, corner), (2, height, breadth))
        contribution = (
            row_strength[:, None] * col_strength[None, :] * shifted
            - 0.5 * (row_outflow[:, None] + col_outflow[None, :]) * matrix
        )
        summed = summed + jnp.where(jump_slot < active, contribution, 0.0)
    return summed


def diagonal_sum(matrix, row_first, col_first):
    row_index = lax.broadcasted_iota(jnp.int32, matrix.shape, 0) + row_first
    col_index = lax.broadcasted_iota(jnp.int32, matrix.shape, 1) + col_first
    return jnp.sum(jnp.where(row_index == col_index, matrix, 0.0))


def local(rho_real, rho_imag, hamiltonian, amplitudes, offsets, active_jumps):
    height, breadth = rho_real.shape
    levels = amplitudes.shape[1]
    row_first = lax.axis_index("row") * height
    col_first = lax.axis_index("col") * breadth
    active = active_jumps[0]
    ham_columns = lax.all_gather(hamiltonian, "row", axis=0, tiled=True)
    start_trace = lax.psum(diagonal_sum(rho_real, row_first, col_first), ("row", "col"))

    def drift(real_part, imag_part):
        real_low = real_part.astype(jnp.bfloat16)
        imag_low = imag_part.astype(jnp.bfloat16)
        row_panel = lax.all_gather(hamiltonian, "col", axis=1, tiled=True)
        pieces = (
            lax.all_gather(real_low, "row", axis=0, tiled=True),
            lax.all_gather(imag_low, "row", axis=0, tiled=True),
        )
        strip = row_panel
        left_real = jnp.dot(strip, pieces[0], preferred_element_type=jnp.float32)
        left_imag = jnp.dot(strip, pieces[1], preferred_element_type=jnp.float32)
        pieces = (
            lax.all_gather(real_low, "col", axis=1, tiled=True),
            lax.all_gather(imag_low, "col", axis=1, tiled=True),
        )
        strip = ham_columns
        right_real = jnp.dot(pieces[0], strip, preferred_element_type=jnp.float32)
        right_imag = jnp.dot(pieces[1], strip, preferred_element_type=jnp.float32)
        matrix = jnp.stack([real_part, imag_part])
        padded = extended(matrix.astype(jnp.bfloat16), (("row", 1), ("col", 2)), OMAX).astype(
            matrix.dtype
        )
        loss = dissipate(matrix, padded, amplitudes, offsets, active, row_first, col_first)
        return (left_imag - right_imag + loss[0], right_real - left_real + loss[1])

    first_real, first_imag = drift(rho_real, rho_imag)
    middle_real = rho_real + step_size * first_real
    middle_imag = rho_imag + step_size * first_imag
    rescale = levels / start_trace
    middle_real = middle_real * rescale
    middle_imag = middle_imag * rescale
    second_real, second_imag = drift(middle_real, middle_imag)
    updated_real = rho_real + 0.5 * step_size * (first_real + second_real)
    updated_imag = rho_imag + 0.5 * step_size * (first_imag + second_imag)
    rescale = levels / start_trace
    return (updated_real * rescale, updated_imag * rescale)


def solution(mesh):
    in_specs = (P("row", "col"), P("row", "col"), P("row", "col"), P(), P(), P())
    out_specs = (P("row", "col"), P("row", "col"))
    return jax.shard_map(local, mesh=mesh, in_specs=in_specs, out_specs=out_specs, check_vma=False)
```

profile of v0, /device:TPU:0, one launch (start us, length us, event | category | flops | bytes accessed | tf_op | source)
XLA Modules:
  0.0 739.0 jit_solution(2727342368948847065)
XLA Ops:
  7.2 2.7 convert_element_type.41
  10.0 0.7 all-gather.11.cloned.1.call-update
  12.1 2.0 fusion.1
  14.1 1.3 copy-done.4
  15.4 4.9 collective-permute-start
  20.4 1.3 collective-permute-start.1
  39.6 2.4 add_multiply_fusion.2
  41.9 2.3 add_multiply_fusion.4
  44.3 2.4 add_multiply_fusion.6
  46.7 2.3 add_multiply_fusion.8
  49.0 2.4 broadcast_multiply_fusion
  51.3 2.4 broadcast_multiply_fusion.2
  53.7 2.5 broadcast_multiply_fusion.4
  56.2 1.3 select_reduce_fusion
  58.1 1.5 collective-permute-start.2
  59.8 1.3 collective-permute-start.3
  61.1 2.4 broadcast_multiply_fusion.6
  63.5 47.8 %psum.7 = f32[]{:T(128)} all-reduce(f32[]{:T(128)} %select_reduce_fusion), channel_id=1, replica_groups=mesh['row'=4,'col'=8] {'row','col'}, use_global_device_ids=true, to_apply=%region_1.2 | all-reduce | flops 1 | bytes 8 | tf_op jit(solution)/shard_map/psum | solution.py:67
  128.4 5.1 maximum_convert_fusion
  133.5 28.7 %select_add_fusion.1 = f32[2,1024,512]{2,1,0:T(8,128)} fusion(f32[2,1056,544]{2,1,0:T(8,128)} %maximum_convert_fusion, s32[]{:T(128)S(6)} %select_n.358, s32[]{:T(128)S(6)} %select_n.359, s32[]{:T(128)S(6)} %select_n.351, s32[]{:T(128)S(6)} %select_n.352, s32[]{:T(128)S(6)} %select_n.344, s32[]{:T(128)S(6)} %select_n.345, s32[]{:T(128)S(6)} %select_n.337, ...), kind=kLoop, calls=%fused_computation.3 | loop fusion | flops 41943040 | bytes 75497544 | tf_op jit(solution)/shard_map/add | solution.py:50
  162.2 10.7 %fusion.70 = f32[1024,512]{1,0:T(8,128)} fusion(bf16[1024,4096]{1,0:T(8,128)(2,1)} %all-gather.11.cloned.1.call-done, bf16[4096,512]{1,0:T(8,128)(2,1)} %all-gather.13.cloned.1.call-done), kind=kOutput, calls=%fused_computation.125 | convolution fusion | flops 4294967296 | bytes 14680064 | tf_op jit(solution)/shard_map/dot_general | solution.py:79
  172.9 61.1 %all-gather.17.cloned.1.call-done = bf16[4096,512]{1,0:T(8,128)(2,1)} async-done(((bf16[1024,512]{1,0:T(8,128)(2,1)}), bf16[4096,512]{1,0:T(8,128)(2,1)}) %all-gather.17.cloned.1.call-update) | async-done | bytes 4194320 | tf_op jit(solution)/shard_map/all_gather | solution.py:66
  234.0 56.1 %all-gather.15.cloned.1.call-done = bf16[1024,4096]{1,0:T(8,128)(2,1)} async-done(((bf16[1024,512]{1,0:T(8,128)(2,1)}), bf16[1024,4096]{1,0:T(8,128)(2,1)}) %all-gather.15.cloned.1.call-update) | async-done | bytes 8388624 | tf_op jit(solution)/shard_map/all_gather | solution.py:82
  290.2 10.5 %fusion.13 = f32[1024,512]{1,0:T(8,128)S(1)} fusion(f32[2,1024,512]{2,1,0:T(8,128)} %select_add_fusion.1, f32[1024,512]{1,0:T(8,128)} %fusion.70, bf16[1024,4096]{1,0:T(8,128)(2,1)} %all-gather.15.cloned.1.call-done, bf16[4096,512]{1,0:T(8,128)(2,1)} %all-gather.17.cloned.1.call-done), kind=kOutput, calls=%fused_computation.23 | convolution fusion | flops 4296015872 | bytes 18874368 | tf_op jit(solution)/shard_map/dot_general | solution.py:86
  300.6 2.7 fusion.16
  305.7 53.7 %all-gather.19.cloned.1.call-done = bf16[1024,4096]{1,0:T(8,128)(2,1)} async-done(((bf16[1024,512]{1,0:T(8,128)(2,1)}), bf16[1024,4096]{1,0:T(8,128)(2,1)}) %all-gather.19.cloned.1.call-update) | async-done | bytes 8388624 | tf_op jit(solution)/shard_map/all_gather | solution.py:81
  359.4 10.5 %fusion.71 = f32[1024,512]{1,0:T(8,128)} fusion(bf16[1024,4096]{1,0:T(8,128)(2,1)} %all-gather.19.cloned.1.call-done, bf16[4096,512]{1,0:T(8,128)(2,1)} %all-gather.17.cloned.1.call-done), kind=kOutput, calls=%fused_computation.126 | convolution fusion | flops 4294967296 | bytes 14680064 | tf_op jit(solution)/shard_map/dot_general | solution.py:85
  369.8 71.7 %all-gather.21.cloned.1.call-done = bf16[4096,512]{1,0:T(8,128)(2,1)} async-done(((bf16[1024,512]{1,0:T(8,128)(2,1)}), bf16[4096,512]{1,0:T(8,128)(2,1)}) %all-gather.21.cloned.1.call-update) | async-done | bytes 4194320 | tf_op jit(solution)/shard_map/all_gather | solution.py:74
  441.6 10.3 %fusion.12 = f32[1024,512]{1,0:T(8,128)S(1)} fusion(f32[2,1024,512]{2,1,0:T(8,128)} %select_add_fusion.1, f32[1024,512]{1,0:T(8,128)} %fusion.71, bf16[1024,4096]{1,0:T(8,128)(2,1)} %all-gather.11.cloned.1.call-done, bf16[4096,512]{1,0:T(8,128)(2,1)} %all-gather.21.cloned.1.call-done), kind=kOutput, calls=%fused_computation.21 | convolution fusion | flops 4296015872 | bytes 18874368 | tf_op jit(solution)/shard_map/dot_general | solution.py:78
  451.9 2.5 fusion.15
  454.5 2.6 fusion
  457.1 1.3 copy-done.6
  458.4 1.3 collective-permute-start.4
  459.7 1.3 collective-permute-start.5
  461.3 4.3 collective-permute-done.5
  465.6 1.5 pad_maximum_fusion.4
  467.3 1.3 collective-permute-start.6
  468.8 1.3 collective-permute-start.7
  470.1 27.8 %all-gather.27.cloned.1.call-done = bf16[1024,4096]{1,0:T(8,128)(2,1)} async-done(((bf16[1024,512]{1,0:T(8,128)(2,1)}), bf16[1024,4096]{1,0:T(8,128)(2,1)}) %all-gather.27.cloned.1.call-update) | async-done | bytes 8388624 | tf_op jit(solution)/shard_map/all_gather | solution.py:81
  497.9 10.4 %fusion.73 = f32[1024,512]{1,0:T(8,128)} fusion(bf16[1024,4096]{1,0:T(8,128)(2,1)} %all-gather.27.cloned.1.call-done, bf16[4096,512]{1,0:T(8,128)(2,1)} %all-gather.17.cloned.1.call-done), kind=kOutput, calls=%fused_computation.128 | convolution fusion | flops 4294967296 | bytes 14680064 | tf_op jit(solution)/shard_map/dot_general | solution.py:85
  508.9 5.4 maximum_convert_fusion.1
  514.3 29.5 %select_add_fusion = f32[2,1024,512]{2,1,0:T(8,128)} fusion(f32[2,1056,544]{2,1,0:T(8,128)} %maximum_convert_fusion.1, s32[]{:T(128)S(6)} %select_n.358, s32[]{:T(128)S(6)} %select_n.359, s32[]{:T(128)S(6)} %select_n.351, s32[]{:T(128)S(6)} %select_n.352, s32[]{:T(128)S(6)} %select_n.344, s32[]{:T(128)S(6)} %select_n.345, s32[]{:T(128)S(6)} %select_n.337, ...), kind=kLoop, calls=%fused_computation.2 | loop fusion | flops 41943040 | bytes 75497544 | tf_op jit(solution)/shard_map/add | solution.py:50
  543.7 37.2 %all-gather.29.cloned.1.call-done = bf16[4096,512]{1,0:T(8,128)(2,1)} async-done(((bf16[1024,512]{1,0:T(8,128)(2,1)}), bf16[4096,512]{1,0:T(8,128)(2,1)}) %all-gather.29.cloned.1.call-update) | async-done | bytes 4194320 | tf_op jit(solution)/shard_map/all_gather | solution.py:74
  580.9 12.5 %fusion.6 = f32[1024,512]{1,0:T(8,128)} fusion(f32[1024,512]{1,0:T(8,128)S(1)} %copy-done, f32[1024,512]{1,0:T(8,128)} %copy-done.8, f32[2,1024,512]{2,1,0:T(8,128)} %select_add_fusion, f32[1024,512]{1,0:T(8,128)} %fusion.73, bf16[1024,4096]{1,0:T(8,128)(2,1)} %all-gather.11.cloned.1.call-done, bf16[4096,512]{1,0:T(8,128)(2,1)} %all-gather.29.cloned.1.call-done, ...), kind=kOutput, calls=%fused_computation.13 | convolution fusion | flops 4298113024 | bytes 23068676 | tf_op jit(solution)/shard_map/dot_general | solution.py:78
  593.4 43.8 %all-gather.25.cloned.1.call-done = bf16[1024,4096]{1,0:T(8,128)(2,1)} async-done(((bf16[1024,512]{1,0:T(8,128)(2,1)}), bf16[1024,4096]{1,0:T(8,128)(2,1)}) %all-gather.25.cloned.1.call-update) | async-done | bytes 8388624 | tf_op jit(solution)/shard_map/all_gather | solution.py:82
  637.2 10.5 %fusion.72 = f32[1024,512]{1,0:T(8,128)} fusion(bf16[1024,4096]{1,0:T(8,128)(2,1)} %all-gather.25.cloned.1.call-done, bf16[4096,512]{1,0:T(8,128)(2,1)} %all-gather.17.cloned.1.call-done), kind=kOutput, calls=%fused_computation.127 | convolution fusion | flops 4294967296 | bytes 14680064 | tf_op jit(solution)/shard_map/dot_general | solution.py:86
  647.7 71.7 %all-gather.23.cloned.1.call-done = bf16[4096,512]{1,0:T(8,128)(2,1)} async-done(((bf16[1024,512]{1,0:T(8,128)(2,1)}), bf16[4096,512]{1,0:T(8,128)(2,1)}) %all-gather.23.cloned.1.call-update) | async-done | bytes 4194320 | tf_op jit(solution)/shard_map/all_gather | solution.py:75
  719.4 12.5 %fusion.11 = f32[1024,512]{1,0:T(8,128)} fusion(f32[1024,512]{1,0:T(8,128)S(1)} %copy-done.3, f32[1024,512]{1,0:T(8,128)} %copy-done.7, f32[2,1024,512]{2,1,0:T(8,128)} %select_add_fusion, f32[1024,512]{1,0:T(8,128)} %fusion.72, bf16[1024,4096]{1,0:T(8,128)(2,1)} %all-gather.11.cloned.1.call-done, bf16[4096,512]{1,0:T(8,128)(2,1)} %all-gather.23.cloned.1.call-done, ...), kind=kOutput, calls=%fused_computation.19 | convolution fusion | flops 4298113024 | bytes 23068676 | tf_op jit(solution)/shard_map/dot_general | solution.py:79
  (103 shorter events, 14.1 us)
Async XLA Ops:
  7.2 155.0 %all-gather.13.cloned.1.call-start = ((), (), s32[]{:S(2)}) async-start(), calls=%async_computation.1 | async-start | bytes 5242880 | tf_op jit(solution)/shard_map/all_gather | solution.py:75
  9.9 2.1 copy-start
  10.0 152.2 %all-gather.11.cloned.1.call-start = ((), (), s32[]{:S(2)}) async-start(), calls=%async_computation | async-start | bytes 9437184 | tf_op jit(solution)/shard_map/all_gather | solution.py:72
  10.7 223.3 %all-gather.17.cloned.1.call-start = ((), (), s32[]{:S(2)}) async-start(), calls=%async_computation.3 | async-start | bytes 5242880 | tf_op jit(solution)/shard_map/all_gather | solution.py:66
  11.4 278.7 %all-gather.15.cloned.1.call-start = ((), (), s32[]{:S(2)}) async-start(), calls=%async_computation.2 | async-start | bytes 9437184 | tf_op jit(solution)/shard_map/all_gather | solution.py:82
  12.0 347.3 %all-gather.19.cloned.1.call-start = ((), (), s32[]{:S(2)}) async-start(), calls=%async_computation.4 | async-start | bytes 9437184 | tf_op jit(solution)/shard_map/all_gather | solution.py:81
  12.1 9.6 %copy-start.10 = (s32[8]{0:T(128)S(1)}, s32[8]{0:T(128)}, u32[]{:S(2)}) copy-start(s32[8]{0:T(128)} %param.10) | copy-start | bytes 100
  12.1 20.4 %copy-start.9 = (f32[8,4096]{1,0:T(8,128)S(1)}, f32[8,4096]{1,0:T(8,128)}, u32[]{:S(2)}) copy-start(f32[8,4096]{1,0:T(8,128)} %param.9) | copy-start | bytes 393220
  14.1 1.3 copy-start.4
  15.4 42.2 %collective-permute-start = (bf16[2,16,512]{2,1,0:T(8,128)(2,1)S(1)}, bf16[2,16,512]{2,1,0:T(8,128)(2,1)S(1)}, u32[]{:S(2)}, u32[]{:S(2)}) collective-permute-start(bf16[2,16,512]{2,1,0:T(8,128)(2,1)S(1)} %get-tuple-element.29), channel_id=1, source_target_pairs={{0,8},{8,16},{16,24},{1,9},{9,17},{17,25},{2,10},{10,18},{18,26},{... | collective-permute-start | bytes 98312 | tf_op jit(solution)/shard_map/ppermute | solution.py:18
  20.4 37.3 %collective-permute-start.1 = (bf16[2,16,512]{2,1,0:T(8,128)(2,1)S(1)}, bf16[2,16,512]{2,1,0:T(8,128)(2,1)S(1)}, u32[]{:S(2)}, u32[]{:S(2)}) collective-permute-start(bf16[2,16,512]{2,1,0:T(8,128)(2,1)S(1)} %get-tuple-element.30), channel_id=1, source_target_pairs={{8,0},{16,8},{24,16},{9,1},{17,9},{25,17},{10,2},{18,10},{26,18},{... | collective-permute-start | bytes 98312 | tf_op jit(solution)/shard_map/ppermute | solution.py:20
  53.7 2.5 copy-start.1
  53.7 3.9 copy-start.5
  58.1 69.7 %collective-permute-start.2 = (bf16[2,1056,16]{1,2,0:T(8,128)(2,1)S(1)}, bf16[2,1056,16]{1,2,0:T(8,128)(2,1)S(1)}, u32[]{:S(2)}, u32[]{:S(2)}) collective-permute-start(bf16[2,1056,16]{1,2,0:T(8,128)(2,1)S(1)} %copy.10), channel_id=1, source_target_pairs={{0,1},{1,2},{2,3},{3,4},{4,5},{5,6},{6,7},{8,9},{9,10},{10,11},{11... | collective-permute-start | bytes 202760 | tf_op jit(solution)/shard_map/ppermute | solution.py:18
  59.8 68.3 %collective-permute-start.3 = (bf16[2,1056,16]{1,2,0:T(8,128)(2,1)S(1)}, bf16[2,1056,16]{1,2,0:T(8,128)(2,1)S(1)}, u32[]{:S(2)}, u32[]{:S(2)}) collective-permute-start(bf16[2,1056,16]{1,2,0:T(8,128)(2,1)S(1)} %copy.11), channel_id=1, source_target_pairs={{1,0},{2,1},{3,2},{4,3},{5,4},{6,5},{7,6},{9,8},{10,9},{11,10},{12... | collective-permute-start | bytes 202760 | tf_op jit(solution)/shard_map/ppermute | solution.py:20
  290.1 10.5 %copy-start.2 = (f32[1024,512]{1,0:T(8,128)S(1)}, f32[1024,512]{1,0:T(8,128)}, u32[]{:S(2)}) copy-start(f32[1024,512]{1,0:T(8,128)} %param.6) | copy-start | bytes 6291460
  300.6 2.7 copy-start.7
  303.4 138.2 %all-gather.21.cloned.1.call-start = ((), (), s32[]{:S(2)}) async-start(), calls=%async_computation.5 | async-start | bytes 5242880 | tf_op jit(solution)/shard_map/all_gather | solution.py:74
  303.9 194.0 %all-gather.27.cloned.1.call-start = ((), (), s32[]{:S(2)}) async-start(), calls=%async_computation.8 | async-start | bytes 9437184 | tf_op jit(solution)/shard_map/all_gather | solution.py:81
  304.7 276.3 %all-gather.29.cloned.1.call-start = ((), (), s32[]{:S(2)}) async-start(), calls=%async_computation.9 | async-start | bytes 5242880 | tf_op jit(solution)/shard_map/all_gather | solution.py:74
  305.4 331.8 %all-gather.25.cloned.1.call-start = ((), (), s32[]{:S(2)}) async-start(), calls=%async_computation.7 | async-start | bytes 9437184 | tf_op jit(solution)/shard_map/all_gather | solution.py:82
  451.9 2.5 copy-start.8
  454.4 265.0 %all-gather.23.cloned.1.call-start = ((), (), s32[]{:S(2)}) async-start(), calls=%async_computation.6 | async-start | bytes 5242880 | tf_op jit(solution)/shard_map/all_gather | solution.py:75
  457.1 1.3 copy-start.6
  458.4 2.9 collective-permute-start.4
  459.7 5.9 collective-permute-start.5
  467.3 41.0 %collective-permute-start.6 = (bf16[2,1056,16]{1,2,0:T(8,128)(2,1)S(1)}, bf16[2,1056,16]{1,2,0:T(8,128)(2,1)S(1)}, u32[]{:S(2)}, u32[]{:S(2)}) collective-permute-start(bf16[2,1056,16]{1,2,0:T(8,128)(2,1)S(1)} %copy.15), channel_id=1, source_target_pairs={{0,1},{1,2},{2,3},{3,4},{4,5},{5,6},{6,7},{8,9},{9,10},{10,11},{11... | collective-permute-start | bytes 202760 | tf_op jit(solution)/shard_map/ppermute | solution.py:18
  468.8 39.8 %collective-permute-start.7 = (bf16[2,1056,16]{1,2,0:T(8,128)(2,1)S(1)}, bf16[2,1056,16]{1,2,0:T(8,128)(2,1)S(1)}, u32[]{:S(2)}, u32[]{:S(2)}) collective-permute-start(bf16[2,1056,16]{1,2,0:T(8,128)(2,1)S(1)} %copy.16), channel_id=1, source_target_pairs={{1,0},{2,1},{3,2},{4,3},{5,4},{6,5},{7,6},{9,8},{10,9},{11,10},{12... | collective-permute-start | bytes 202760 | tf_op jit(solution)/shard_map/ppermute | solution.py:20
  593.4 126.0 %copy-start.3 = (f32[1024,512]{1,0:T(8,128)S(1)}, f32[1024,512]{1,0:T(8,128)}, u32[]{:S(2)}) copy-start(f32[1024,512]{1,0:T(8,128)} %param.6) | copy-start | bytes 6291460
Sparse Core Ops, SparseCore 0:
  10.1 84.7 all-gather.12
  96.7 54.9 all-gather.10
  153.3 80.7 all-gather.16
  235.8 54.3 all-gather.14
  303.5 55.8 all-gather.18
  360.8 80.7 all-gather.20
  443.4 54.4 all-gather.26
  499.5 81.4 all-gather.28
  582.8 54.3 all-gather.24
  638.6 80.7 all-gather.22
where the time goes:
time: 744 us; the launch traced here: 739 us
  waiting for transfers between devices  432 us (58%)
  other arithmetic  108 us (15%)
  matrix products  87.7 us (12%)
  blocking collectives  47.8 us (6%)
  between operations  41.4 us (6%)
  starting transfers between devices  14.7 us (2%)
    all_gather x2, waiting for transfers between devices, drift(): lax.all_gather(real_low, 'row', axis=0, tiled=True)  109 us
    all_gather x2, waiting for transfers between devices, drift(): lax.all_gather(imag_low, 'col', axis=1, tiled=True)  99.9 us
    all_gather x2, waiting for transfers between devices, drift(): lax.all_gather(real_low, 'col', axis=1, tiled=True)  81.5 us
    all_gather x2, waiting for transfers between devices, drift(): lax.all_gather(imag_low, 'row', axis=0, tiled=True)  71.7 us
    all_gather x1, waiting for transfers between devices, local(): ham_columns = lax.all_gather(hamiltonian, 'row', axis=0, tiled=True)  61.1 us
    add x2, other arithmetic, dissipate(): summed = summed + jnp.where(jump_slot < active, contribution, 0.0)  58.1 us
    psum x1, blocking collectives, local(): lax.psum(diagonal_sum(rho_real, row_first, col_first), ('row', 'col'))  47.8 us
    dot_general x2, matrix products, drift(): left_imag = jnp.dot(strip, pieces[1], preferred_element_type=jnp.float32)  23.2 us
  transfers between devices with their start and end apart: 18, of which 10 were waited for; matrix products, arithmetic and copies ran while one was open for 23% of the time, Pallas kernels for 0%

commit v1 on v0

--- a/solution.py
+++ b/solution.py
@@ -64,7 +64,8 @@
     col_first = lax.axis_index("col") * breadth
     active = active_jumps[0]
     ham_columns = lax.all_gather(hamiltonian, "row", axis=0, tiled=True)
-    start_trace = lax.psum(diagonal_sum(rho_real, row_first, col_first), ("row", "col"))
+    half = lax.psum(diagonal_sum(rho_real, row_first, col_first), "col")
+    start_trace = lax.psum(half, "row")
 
     def drift(real_part, imag_part):
         real_low = real_part.astype(jnp.bfloat16)

time: 744 us -> 744 us (level)
  blocking collectives: 47.8 us -> 29.2 us
  waiting for transfers between devices: 432 us -> 446 us
    psum x1 -> x2, blocking collectives: 47.8 us -> 29.2 us  [the longest x1 14.9 us: local(): half = lax.psum(diagonal_sum(rho_real, row_first, col_first), 'col')]
    all_gather x1, waiting for transfers between devices: 61.1 us -> 72 us  [local(): ham_columns = lax.all_gather(hamiltonian, 'row', axis=0, tiled=True)]
  transfers between devices with their start and end apart: 18 -> 18, of which waited for: 10 -> 11; matrix products, arithmetic and copies ran while one was open for 23% -> 24% of each run, Pallas kernels for 0% -> 0%
where the time goes in v1:
time: 744 us; the launch traced here: 738 us
  waiting for transfers between devices  446 us (60%)
  other arithmetic  112 us (15%)
  matrix products  87.4 us (12%)
  between operations  41.8 us (6%)
  blocking collectives  29.2 us (4%)
  starting transfers between devices  14.5 us (2%)
    all_gather x2, waiting for transfers between devices, drift(): lax.all_gather(real_low, 'row', axis=0, tiled=True)  109 us
    all_gather x2, waiting for transfers between devices, drift(): lax.all_gather(imag_low, 'col', axis=1, tiled=True)  99.9 us
    all_gather x2, waiting for transfers between devices, drift(): lax.all_gather(real_low, 'col', axis=1, tiled=True)  81.5 us
    all_gather x1, waiting for transfers between devices, local(): ham_columns = lax.all_gather(hamiltonian, 'row', axis=0, tiled=True)  72 us
    all_gather x2, waiting for transfers between devices, drift(): lax.all_gather(imag_low, 'row', axis=0, tiled=True)  71.7 us
    add x2, other arithmetic, dissipate(): summed = summed + jnp.where(jump_slot < active, contribution, 0.0)  58.8 us
    dot_general x2, matrix products, drift(): left_imag = jnp.dot(strip, pieces[1], preferred_element_type=jnp.float32)  22.8 us
    dot_general x2, matrix products, drift(): left_real = jnp.dot(strip, pieces[0], preferred_element_type=jnp.float32)  22.8 us
  transfers between devices with their start and end apart: 18, of which 11 were waited for; matrix products, arithmetic and copies ran while one was open for 24% of the time, Pallas kernels for 0%

profile of v1, /device:TPU:0, one launch (start us, length us, event | category | flops | bytes accessed | tf_op | source)
XLA Modules:
  0.0 737.9 jit_solution(15006518212551161721)
XLA Ops:
  7.2 2.7 convert_element_type.41
  12.1 2.0 fusion.1
  14.1 1.3 copy-done.3
  15.4 4.9 collective-permute-start
  20.4 1.3 collective-permute-start.1
  39.8 2.9 select_reduce_fusion
  42.7 2.4 add_multiply_fusion.2
  45.1 2.4 add_multiply_fusion.4
  47.5 2.3 add_multiply_fusion.6
  49.8 2.4 add_multiply_fusion.8
  52.2 2.4 broadcast_multiply_fusion
  54.5 2.4 broadcast_multiply_fusion.2
  56.9 2.4 broadcast_multiply_fusion.4
  59.3 14.9 %psum.14 = f32[]{:T(128)} all-reduce(f32[]{:T(128)} %select_reduce_fusion), channel_id=1, replica_groups=mesh['row'=4,'col'=8] {'col'}, use_global_device_ids=true, to_apply=%region_1.2 | all-reduce | flops 1 | bytes 8 | tf_op jit(solution)/shard_map/psum | solution.py:67
  74.3 1.5 pad_maximum_fusion.7
  76.0 1.3 collective-permute-start.2
  77.5 1.3 collective-permute-start.3
  78.8 2.4 broadcast_multiply_fusion.6
  81.3 14.3 %psum.15 = f32[]{:T(128)} all-reduce(f32[]{:T(128)} %psum.14), channel_id=1, replica_groups=mesh['row'=4,'col'=8] {'row'}, use_global_device_ids=true, to_apply=%region_2.3 | all-reduce | flops 1 | bytes 8 | tf_op jit(solution)/shard_map/psum | solution.py:68
  112.9 5.1 maximum_convert_fusion
  118.0 29.2 %select_add_fusion.1 = f32[2,1024,512]{2,1,0:T(8,128)} fusion(f32[2,1056,544]{2,1,0:T(8,128)} %maximum_convert_fusion, s32[]{:T(128)S(6)} %select_n.358, s32[]{:T(128)S(6)} %select_n.359, s32[]{:T(128)S(6)} %select_n.351, s32[]{:T(128)S(6)} %select_n.352, s32[]{:T(128)S(6)} %select_n.344, s32[]{:T(128)S(6)} %select_n.345, s32[]{:T(128)S(6)} %select_n.337, ...), kind=kLoop, calls=%fused_computation.3 | loop fusion | flops 41943040 | bytes 75497544 | tf_op jit(solution)/shard_map/add | solution.py:50
  147.3 3.4 all-gather.11.cloned.1.call-done
  150.7 10.4 %fusion.70 = f32[1024,512]{1,0:T(8,128)} fusion(bf16[1024,4096]{1,0:T(8,128)(2,1)} %all-gather.11.cloned.1.call-done, bf16[4096,512]{1,0:T(8,128)(2,1)} %all-gather.13.cloned.1.call-done), kind=kOutput, calls=%fused_computation.125 | convolution fusion | flops 4294967296 | bytes 14680064 | tf_op jit(solution)/shard_map/dot_general | solution.py:80
  161.1 72.0 %all-gather.17.cloned.1.call-done = bf16[4096,512]{1,0:T(8,128)(2,1)} async-done(((bf16[1024,512]{1,0:T(8,128)(2,1)}), bf16[4096,512]{1,0:T(8,128)(2,1)}) %all-gather.17.cloned.1.call-update) | async-done | bytes 4194320 | tf_op jit(solution)/shard_map/all_gather | solution.py:66
  233.0 56.1 %all-gather.15.cloned.1.call-done = bf16[1024,4096]{1,0:T(8,128)(2,1)} async-done(((bf16[1024,512]{1,0:T(8,128)(2,1)}), bf16[1024,4096]{1,0:T(8,128)(2,1)}) %all-gather.15.cloned.1.call-update) | async-done | bytes 8388624 | tf_op jit(solution)/shard_map/all_gather | solution.py:83
  289.1 10.5 %fusion.13 = f32[1024,512]{1,0:T(8,128)S(1)} fusion(f32[2,1024,512]{2,1,0:T(8,128)} %select_add_fusion.1, f32[1024,512]{1,0:T(8,128)} %fusion.70, bf16[1024,4096]{1,0:T(8,128)(2,1)} %all-gather.15.cloned.1.call-done, bf16[4096,512]{1,0:T(8,128)(2,1)} %all-gather.17.cloned.1.call-done), kind=kOutput, calls=%fused_computation.23 | convolution fusion | flops 4296015872 | bytes 18874368 | tf_op jit(solution)/shard_map/dot_general | solution.py:87
  299.6 2.7 fusion.16
  304.6 53.7 %all-gather.19.cloned.1.call-done = bf16[1024,4096]{1,0:T(8,128)(2,1)} async-done(((bf16[1024,512]{1,0:T(8,128)(2,1)}), bf16[1024,4096]{1,0:T(8,128)(2,1)}) %all-gather.19.cloned.1.call-update) | async-done | bytes 8388624 | tf_op jit(solution)/shard_map/all_gather | solution.py:82
  358.3 10.4 %fusion.71 = f32[1024,512]{1,0:T(8,128)} fusion(bf16[1024,4096]{1,0:T(8,128)(2,1)} %all-gather.19.cloned.1.call-done, bf16[4096,512]{1,0:T(8,128)(2,1)} %all-gather.17.cloned.1.call-done), kind=kOutput, calls=%fused_computation.126 | convolution fusion | flops 4294967296 | bytes 14680064 | tf_op jit(solution)/shard_map/dot_general | solution.py:86
  368.8 71.7 %all-gather.21.cloned.1.call-done = bf16[4096,512]{1,0:T(8,128)(2,1)} async-done(((bf16[1024,512]{1,0:T(8,128)(2,1)}), bf16[4096,512]{1,0:T(8,128)(2,1)}) %all-gather.21.cloned.1.call-update) | async-done | bytes 4194320 | tf_op jit(solution)/shard_map/all_gather | solution.py:75
  440.5 10.3 %fusion.12 = f32[1024,512]{1,0:T(8,128)S(1)} fusion(f32[2,1024,512]{2,1,0:T(8,128)} %select_add_fusion.1, f32[1024,512]{1,0:T(8,128)} %fusion.71, bf16[1024,4096]{1,0:T(8,128)(2,1)} %all-gather.11.cloned.1.call-done, bf16[4096,512]{1,0:T(8,128)(2,1)} %all-gather.21.cloned.1.call-done), kind=kOutput, calls=%fused_computation.21 | convolution fusion | flops 4296015872 | bytes 18874368 | tf_op jit(solution)/shard_map/dot_general | solution.py:79
  450.9 2.5 fusion.15
  453.5 2.6 fusion
  456.1 1.3 copy-done.4
  458.7 1.3 collective-permute-start.5
  460.3 4.3 collective-permute-done.5
  464.6 1.5 pad_maximum_fusion.4
  467.8 1.3 collective-permute-start.7
  469.1 27.8 %all-gather.27.cloned.1.call-done = bf16[1024,4096]{1,0:T(8,128)(2,1)} async-done(((bf16[1024,512]{1,0:T(8,128)(2,1)}), bf16[1024,4096]{1,0:T(8,128)(2,1)}) %all-gather.27.cloned.1.call-update) | async-done | bytes 8388624 | tf_op jit(solution)/shard_map/all_gather | solution.py:82
  496.9 10.4 %fusion.73 = f32[1024,512]{1,0:T(8,128)} fusion(bf16[1024,4096]{1,0:T(8,128)(2,1)} %all-gather.27.cloned.1.call-done, bf16[4096,512]{1,0:T(8,128)(2,1)} %all-gather.17.cloned.1.call-done), kind=kOutput, calls=%fused_computation.128 | convolution fusion | flops 4294967296 | bytes 14680064 | tf_op jit(solution)/shard_map/dot_general | solution.py:86
  507.9 5.4 maximum_convert_fusion.1
  513.2 29.5 %select_add_fusion = f32[2,1024,512]{2,1,0:T(8,128)} fusion(f32[2,1056,544]{2,1,0:T(8,128)} %maximum_convert_fusion.1, s32[]{:T(128)S(6)} %select_n.358, s32[]{:T(128)S(6)} %select_n.359, s32[]{:T(128)S(6)} %select_n.351, s32[]{:T(128)S(6)} %select_n.352, s32[]{:T(128)S(6)} %select_n.344, s32[]{:T(128)S(6)} %select_n.345, s32[]{:T(128)S(6)} %select_n.337, ...), kind=kLoop, calls=%fused_computation.2 | loop fusion | flops 41943040 | bytes 75497544 | tf_op jit(solution)/shard_map/add | solution.py:50
  542.8 37.2 %all-gather.29.cloned.1.call-done = bf16[4096,512]{1,0:T(8,128)(2,1)} async-done(((bf16[1024,512]{1,0:T(8,128)(2,1)}), bf16[4096,512]{1,0:T(8,128)(2,1)}) %all-gather.29.cloned.1.call-update) | async-done | bytes 4194320 | tf_op jit(solution)/shard_map/all_gather | solution.py:75
  579.9 12.5 %fusion.6 = f32[1024,512]{1,0:T(8,128)} fusion(f32[1024,512]{1,0:T(8,128)S(1)} %copy-done, f32[1024,512]{1,0:T(8,128)} %copy-done.6, f32[2,1024,512]{2,1,0:T(8,128)} %select_add_fusion, f32[1024,512]{1,0:T(8,128)} %fusion.73, bf16[1024,4096]{1,0:T(8,128)(2,1)} %all-gather.11.cloned.1.call-done, bf16[4096,512]{1,0:T(8,128)(2,1)} %all-gather.29.cloned.1.call-done, ...), kind=kOutput, calls=%fused_computation.13 | convolution fusion | flops 4298113024 | bytes 23068676 | tf_op jit(solution)/shard_map/dot_general | solution.py:79
  592.4 43.8 %all-gather.25.cloned.1.call-done = bf16[1024,4096]{1,0:T(8,128)(2,1)} async-done(((bf16[1024,512]{1,0:T(8,128)(2,1)}), bf16[1024,4096]{1,0:T(8,128)(2,1)}) %all-gather.25.cloned.1.call-update) | async-done | bytes 8388624 | tf_op jit(solution)/shard_map/all_gather | solution.py:83
  636.2 10.5 %fusion.72 = f32[1024,512]{1,0:T(8,128)} fusion(bf16[1024,4096]{1,0:T(8,128)(2,1)} %all-gather.25.cloned.1.call-done, bf16[4096,512]{1,0:T(8,128)(2,1)} %all-gather.17.cloned.1.call-done), kind=kOutput, calls=%fused_computation.127 | convolution fusion | flops 4294967296 | bytes 14680064 | tf_op jit(solution)/shard_map/dot_general | solution.py:87
  646.7 71.7 %all-gather.23.cloned.1.call-done = bf16[4096,512]{1,0:T(8,128)(2,1)} async-done(((bf16[1024,512]{1,0:T(8,128)(2,1)}), bf16[4096,512]{1,0:T(8,128)(2,1)}) %all-gather.23.cloned.1.call-update) | async-done | bytes 4194320 | tf_op jit(solution)/shard_map/all_gather | solution.py:76
  718.4 12.5 %fusion.11 = f32[1024,512]{1,0:T(8,128)} fusion(f32[1024,512]{1,0:T(8,128)S(1)} %copy-done.2, f32[1024,512]{1,0:T(8,128)} %copy-done.5, f32[2,1024,512]{2,1,0:T(8,128)} %select_add_fusion, f32[1024,512]{1,0:T(8,128)} %fusion.72, bf16[1024,4096]{1,0:T(8,128)(2,1)} %all-gather.11.cloned.1.call-done, bf16[4096,512]{1,0:T(8,128)(2,1)} %all-gather.23.cloned.1.call-done, ...), kind=kOutput, calls=%fused_computation.19 | convolution fusion | flops 4298113024 | bytes 23068676 | tf_op jit(solution)/shard_map/dot_general | solution.py:80
  (100 shorter events, 17.2 us)
Async XLA Ops:
  7.2 140.1 %all-gather.13.cloned.1.call-start = ((), (), s32[]{:S(2)}) async-start(), calls=%async_computation.1 | async-start | bytes 5242880 | tf_op jit(solution)/shard_map/all_gather | solution.py:76
  9.9 2.1 copy-start
  10.0 140.7 %all-gather.11.cloned.1.call-start = ((), (), s32[]{:S(2)}) async-start(), calls=%async_computation | async-start | bytes 9437184 | tf_op jit(solution)/shard_map/all_gather | solution.py:73
  10.7 222.3 %all-gather.17.cloned.1.call-start = ((), (), s32[]{:S(2)}) async-start(), calls=%async_computation.3 | async-start | bytes 5242880 | tf_op jit(solution)/shard_map/all_gather | solution.py:66
  11.4 277.7 %all-gather.15.cloned.1.call-start = ((), (), s32[]{:S(2)}) async-start(), calls=%async_computation.2 | async-start | bytes 9437184 | tf_op jit(solution)/shard_map/all_gather | solution.py:83
  12.0 346.3 %all-gather.19.cloned.1.call-start = ((), (), s32[]{:S(2)}) async-start(), calls=%async_computation.4 | async-start | bytes 9437184 | tf_op jit(solution)/shard_map/all_gather | solution.py:82
  12.1 9.6 %copy-start.8 = (s32[8]{0:T(128)S(1)}, s32[8]{0:T(128)}, u32[]{:S(2)}) copy-start(s32[8]{0:T(128)} %param.10) | copy-start | bytes 100
  12.1 20.6 %copy-start.7 = (f32[8,4096]{1,0:T(8,128)S(1)}, f32[8,4096]{1,0:T(8,128)}, u32[]{:S(2)}) copy-start(f32[8,4096]{1,0:T(8,128)} %param.9) | copy-start | bytes 393220
  14.1 1.3 copy-start.3
  15.4 58.9 %collective-permute-start = (bf16[2,16,512]{2,1,0:T(8,128)(2,1)S(1)}, bf16[2,16,512]{2,1,0:T(8,128)(2,1)S(1)}, u32[]{:S(2)}, u32[]{:S(2)}) collective-permute-start(bf16[2,16,512]{2,1,0:T(8,128)(2,1)S(1)} %get-tuple-element.29), channel_id=1, source_target_pairs={{0,8},{8,16},{16,24},{1,9},{9,17},{17,25},{2,10},{10,18},{18,26},{... | collective-permute-start | bytes 98312 | tf_op jit(solution)/shard_map/ppermute | solution.py:18
  20.4 54.0 %collective-permute-start.1 = (bf16[2,16,512]{2,1,0:T(8,128)(2,1)S(1)}, bf16[2,16,512]{2,1,0:T(8,128)(2,1)S(1)}, u32[]{:S(2)}, u32[]{:S(2)}) collective-permute-start(bf16[2,16,512]{2,1,0:T(8,128)(2,1)S(1)} %get-tuple-element.30), channel_id=1, source_target_pairs={{8,0},{16,8},{24,16},{9,1},{17,9},{25,17},{10,2},{18,10},{26,18},{... | collective-permute-start | bytes 98312 | tf_op jit(solution)/shard_map/ppermute | solution.py:20
  76.0 36.3 %collective-permute-start.2 = (bf16[2,1056,16]{1,2,0:T(8,128)(2,1)S(1)}, bf16[2,1056,16]{1,2,0:T(8,128)(2,1)S(1)}, u32[]{:S(2)}, u32[]{:S(2)}) collective-permute-start(bf16[2,1056,16]{1,2,0:T(8,128)(2,1)S(1)} %copy.10), channel_id=1, source_target_pairs={{0,1},{1,2},{2,3},{3,4},{4,5},{5,6},{6,7},{8,9},{9,10},{10,11},{11... | collective-permute-start | bytes 202760 | tf_op jit(solution)/shard_map/ppermute | solution.py:18
  77.5 35.1 %collective-permute-start.3 = (bf16[2,1056,16]{1,2,0:T(8,128)(2,1)S(1)}, bf16[2,1056,16]{1,2,0:T(8,128)(2,1)S(1)}, u32[]{:S(2)}, u32[]{:S(2)}) collective-permute-start(bf16[2,1056,16]{1,2,0:T(8,128)(2,1)S(1)} %copy.11), channel_id=1, source_target_pairs={{1,0},{2,1},{3,2},{4,3},{5,4},{6,5},{7,6},{9,8},{10,9},{11,10},{12... | collective-permute-start | bytes 202760 | tf_op jit(solution)/shard_map/ppermute | solution.py:20
  289.1 10.5 %copy-start.1 = (f32[1024,512]{1,0:T(8,128)S(1)}, f32[1024,512]{1,0:T(8,128)}, u32[]{:S(2)}) copy-start(f32[1024,512]{1,0:T(8,128)} %param.6) | copy-start | bytes 6291460
  299.6 2.7 copy-start.5
  302.3 138.2 %all-gather.21.cloned.1.call-start = ((), (), s32[]{:S(2)}) async-start(), calls=%async_computation.5 | async-start | bytes 5242880 | tf_op jit(solution)/shard_map/all_gather | solution.py:75
  302.9 194.0 %all-gather.27.cloned.1.call-start = ((), (), s32[]{:S(2)}) async-start(), calls=%async_computation.8 | async-start | bytes 9437184 | tf_op jit(solution)/shard_map/all_gather | solution.py:82
  303.7 276.3 %all-gather.29.cloned.1.call-start = ((), (), s32[]{:S(2)}) async-start(), calls=%async_computation.9 | async-start | bytes 5242880 | tf_op jit(solution)/shard_map/all_gather | solution.py:75
  304.4 331.8 %all-gather.25.cloned.1.call-start = ((), (), s32[]{:S(2)}) async-start(), calls=%async_computation.7 | async-start | bytes 9437184 | tf_op jit(solution)/shard_map/all_gather | solution.py:83
  450.9 2.5 copy-start.6
  453.4 264.9 %all-gather.23.cloned.1.call-start = ((), (), s32[]{:S(2)}) async-start(), calls=%async_computation.6 | async-start | bytes 5242880 | tf_op jit(solution)/shard_map/all_gather | solution.py:76
  456.1 1.3 copy-start.4
  457.4 2.9 collective-permute-start.4
  458.7 5.9 collective-permute-start.5
  466.3 41.0 %collective-permute-start.6 = (bf16[2,1056,16]{1,2,0:T(8,128)(2,1)S(1)}, bf16[2,1056,16]{1,2,0:T(8,128)(2,1)S(1)}, u32[]{:S(2)}, u32[]{:S(2)}) collective-permute-start(bf16[2,1056,16]{1,2,0:T(8,128)(2,1)S(1)} %copy.15), channel_id=1, source_target_pairs={{0,1},{1,2},{2,3},{3,4},{4,5},{5,6},{6,7},{8,9},{9,10},{10,11},{11... | collective-permute-start | bytes 202760 | tf_op jit(solution)/shard_map/ppermute | solution.py:18
  467.8 39.8 %collective-permute-start.7 = (bf16[2,1056,16]{1,2,0:T(8,128)(2,1)S(1)}, bf16[2,1056,16]{1,2,0:T(8,128)(2,1)S(1)}, u32[]{:S(2)}, u32[]{:S(2)}) collective-permute-start(bf16[2,1056,16]{1,2,0:T(8,128)(2,1)S(1)} %copy.16), channel_id=1, source_target_pairs={{1,0},{2,1},{3,2},{4,3},{5,4},{6,5},{7,6},{9,8},{10,9},{11,10},{12... | collective-permute-start | bytes 202760 | tf_op jit(solution)/shard_map/ppermute | solution.py:20
  592.4 126.0 %copy-start.2 = (f32[1024,512]{1,0:T(8,128)S(1)}, f32[1024,512]{1,0:T(8,128)}, u32[]{:S(2)}) copy-start(f32[1024,512]{1,0:T(8,128)} %param.6) | copy-start | bytes 6291460
Sparse Core Ops, SparseCore 0:
  10.1 84.2 all-gather.12
  96.3 54.3 all-gather.10
  152.3 80.7 all-gather.16
  234.8 54.3 all-gather.14
  302.4 55.8 all-gather.18
  359.8 80.7 all-gather.20
  442.4 54.4 all-gather.26
  498.5 81.4 all-gather.28
  581.8 54.3 all-gather.24
  637.6 80.7 all-gather.22
